TPU v7x, 32 devices: a whole 2x2x4 slice. The times are simulated.
32 devices in a mesh: grp: 4 (over z), dp: 8 (over y, x, core).
Axes of the slice: x: 2, y: 2, z: 4, core: 2. Of those that a mesh axis runs over, the one named last changes fastest.
Arguments:
- tokens: bfloat16 [4096, 3584], P(('grp', 'dp')), may hold values from -120 to 120, as said below
- lengths: int32 [32, 4], P(('grp', 'dp')), may hold values from 0 to 128, as said below
- dest: int32 [32, 4], P(('grp', 'dp')), may hold values from -1 to 3, as said below
- gain: float32 [3584], replicated, may hold values from 0.5 to 1.5
- weight: bfloat16 [3584, 10240], P('dp', 'grp'), may hold values from -0.09375 to 0.09375
Outputs:
- projected: bfloat16 [2048, 10240], P('dp', 'grp')
Inputs may be any that keep to these rules, and one draw needn't show every extreme that they name: The tokens of one row have a common scale, and so have those of one feature. A device's live rows are the sum of its lengths; rows after them are padding. Within the devices sharing a dp index, live rows fill ceil(live rows / 32) blocks on each device and 8 blocks in all. dest is -1 exactly for a device's blocks past its live rows and an owner along grp otherwise. Within the devices sharing a dp index, every owner receives exactly 2 blocks and no device sends more than 1 block to one owner.
All inputs are finite; a program needn't handle non-finite values.
Results may differ from a plain program's by a relative error of at most 0.0049.
Values may be sent and summed in bfloat16 or wider, within the bound.
A program may use at most 64 MiB of HBM per device.

v0:
```python
import jax
import jax.numpy as jnp
from jax import lax
from jax.sharding import PartitionSpec as P

BLK = 32
OWN_BLK = 2
EPS = 1e-06


def group_layout(dest_all, own_blocks):
    groups, slots_in = dest_all.shape
    flat_dest = dest_all.reshape(-1)
    flat_index = jnp.arange(groups * slots_in, dtype=jnp.int32)
    earlier = flat_index[None, :] < flat_index[:, None]
    same_dest = flat_dest[:, None] == flat_dest[None, :]
    source = flat_index // slots_in
    owner_rank = jnp.sum((same_dest & earlier).astype(jnp.int32), axis=1)
    pair_rank = jnp.sum(
        (same_dest & earlier & (source[:, None] == source[None, :])).astype(jnp.int32), axis=1
    )
    matches = (flat_dest[:, None, None] == jnp.arange(groups, dtype=jnp.int32)[None, :, None]) & (
        owner_rank[:, None, None] == jnp.arange(own_blocks, dtype=jnp.int32)[None, None, :]
    )
    picked = jnp.sum(jnp.where(matches, flat_index[:, None, None], 0), axis=0)
    return (picked, pair_rank)


def block_keys(blocks, lens_all, slots_in):
    doc_ends = jnp.cumsum(lens_all, axis=1)
    source = blocks // slots_in
    within = blocks % slots_in
    offset = jnp.arange(BLK, dtype=jnp.int32)
    position = (within[:, None] * BLK + offset[None, :]).reshape(-1)
    row_source = jnp.broadcast_to(source[:, None], (blocks.shape[0], BLK)).reshape(-1)
    row_ends = doc_ends[row_source]
    doc_index = jnp.sum((position[:, None] >= row_ends).astype(jnp.int32), axis=1)
    is_live = position < row_ends[:, -1]
    doc_keys = row_source * lens_all.shape[1] + doc_index
    slots = lens_all.shape[0] * lens_all.shape[1]
    onehot = (doc_keys[:, None] == jnp.arange(slots, dtype=jnp.int32)[None, :]) & is_live[:, None]
    return onehot


def doc_squares(rows, onehot):
    widened = rows.astype(jnp.float32)
    square = jnp.sum(widened * widened, axis=1)
    return jnp.sum(jnp.where(onehot, square[:, None], 0.0), axis=0)


def apply_scale(rows, onehot, totals, lens_flat, gain):
    features = rows.shape[1]
    mean_square = totals / (jnp.maximum(lens_flat, 1).astype(jnp.float32) * features)
    inverse = lax.rsqrt(mean_square + EPS)
    scale = jnp.sum(jnp.where(onehot, inverse[None, :], 0.0), axis=1)
    return (rows.astype(jnp.float32) * scale[:, None] * gain[None, :]).astype(jnp.bfloat16)


def fold_rows(rows_all, weight):
    return jnp.dot(
        rows_all,
        lax.all_gather(weight, "dp", axis=0, tiled=True),
        preferred_element_type=jnp.float32,
    ).astype(jnp.bfloat16)


def per_device(tokens, lengths, dest, gain, weight):
    groups = lax.axis_size("grp")
    slots_in = 2 * OWN_BLK
    features = tokens.shape[1]
    pair_most = max(1, (slots_in + groups - 1) // groups)
    lens_all, dest_all = (
        lax.all_gather(lengths, "grp", axis=0, tiled=True),
        lax.all_gather(dest, "grp", axis=0, tiled=True),
    )
    lens_flat = lens_all.reshape(-1)
    picked, pair_rank = group_layout(dest_all, OWN_BLK)
    my_index = lax.axis_index("grp")
    my_blocks = lax.dynamic_index_in_dim(picked, my_index, 0, keepdims=False)
    my_dest = dest[0]
    local_index = jnp.arange(slots_in, dtype=jnp.int32)
    my_pair = jnp.sum(
        (
            (my_dest[:, None] == my_dest[None, :]) & (local_index[None, :] < local_index[:, None])
        ).astype(jnp.int32),
        axis=1,
    )
    slot_ids = jnp.arange(groups * pair_most, dtype=jnp.int32)
    send_pick = (my_dest[None, :] == (slot_ids // pair_most)[:, None]) & (
        my_pair[None, :] == (slot_ids % pair_most)[:, None]
    )
    parcel = jnp.dot(
        send_pick.astype(jnp.bfloat16),
        tokens.reshape(slots_in, BLK * features),
        preferred_element_type=jnp.float32,
    ).astype(jnp.bfloat16)
    arrived = lax.all_to_all(parcel, "grp", split_axis=0, concat_axis=0, tiled=True)
    take_slot = my_blocks // slots_in * pair_most + pair_rank[my_blocks]
    take_onehot = (take_slot[:, None] == slot_ids[None, :]).astype(jnp.bfloat16)
    owned_rows = jnp.dot(take_onehot, arrived, preferred_element_type=jnp.float32).astype(
        jnp.bfloat16
    )
    owned_rows = owned_rows.reshape(OWN_BLK * BLK, features)
    raw_all = lax.all_gather(owned_rows, "grp", axis=0, tiled=True)
    group_onehot = block_keys(picked.reshape(-1), lens_all, slots_in)
    group_totals = doc_squares(raw_all, group_onehot)
    rows_all = apply_scale(raw_all, group_onehot, group_totals, lens_flat, gain)
    return fold_rows(rows_all, weight)


def solution(mesh):
    placed = (
        P(("grp", "dp"), None),
        P(("grp", "dp"), None),
        P(("grp", "dp"), None),
        P(),
        P("dp", "grp"),
    )
    return jax.shard_map(
        per_device, mesh=mesh, in_specs=placed, out_specs=P("dp", "grp"), check_vma=False
    )
```

profile of v0, /device:TPU:0, one launch (start us, length us, event | category | flops | bytes accessed | tf_op | source)
XLA Modules:
  0.0 209.6 jit_solution(7032493428231819487)
XLA Ops:
  6.5 0.9 convert_reduce_fusion.3
  7.5 1.9 reshape.291
  9.3 1.3 fusion
  10.6 0.5 broadcast.368
  11.1 1.9 reduce.9
  13.0 0.0 copy-start
  13.0 1.9 reshape.328
  14.9 6.3 %all-to-all-start = ((bf16[4,2,57344]{2,1,0:T(2,128)(2,1)}), bf16[4,2,57344]{2,1,0:T(2,128)(2,1)S(1)}, u32[]{:S(2)}, u32[]{:S(2)}) async-start(bf16[4,2,57344]{2,1,0:T(2,128)(2,1)} %reshape.328), calls=%async_computation | async-start | bytes 1835008 | tf_op jit(solution)/shard_map/all_to_all | solution.py:97
  21.2 0.0 all-gather.5.cloned.1.call-start
  21.2 0.0 copy-done
  21.2 20.8 %all-gather = s32[4,1,4]{2,1,0:T(1,128)S(1)} all-gather(s32[1,1,4]{2,1,0:T(1,128)S(1)} %bitcast.21), channel_id=1, replica_groups=mesh['grp'=4,'dp'=8] {'grp'}, dimensions={0}, use_global_device_ids=true | all-gather | bytes 80 | tf_op jit(solution)/shard_map/all_gather | solution.py:74
  42.0 0.6 broadcast.366
  42.6 0.7 reduce.8
  43.3 0.1 eq.134
  43.4 0.2 convert_reduce_fusion.2
  43.6 0.1 select_reduce_fusion.2
  43.8 0.2 dynamic-slice_reduce_fusion
  44.0 0.6 gather_fusion
  44.7 0.0 all-to-all-done
  44.7 0.9 reshape.329
  45.5 1.3 convolution_convert_fusion.1
  46.8 0.0 copy-start.1
  46.8 1.2 reshape.292
  48.0 0.0 all-gather.5.cloned.1.call-update
  48.1 0.0 all-gather.7.cloned.1.call-start
  48.1 0.7 all-gather.7.cloned.1.call-update
  48.8 0.0 copy-start.2
  48.8 0.0 copy-done.1
  48.8 13.2 %all-gather.1 = s32[4,1,4]{2,1,0:T(1,128)S(1)} all-gather(s32[1,1,4]{2,1,0:T(1,128)S(1)} %bitcast.22), channel_id=1, replica_groups=mesh['grp'=4,'dp'=8] {'grp'}, dimensions={0}, use_global_device_ids=true | all-gather | bytes 80 | tf_op jit(solution)/shard_map/all_gather | solution.py:73
  62.1 0.1 copy.15
  62.2 0.1 reshape.293
  62.3 0.1 iota_add_fusion
  62.3 0.1 add.116
  62.4 0.1 add.121
  62.6 0.2 reduce_window_sum.11
  62.7 0.1 mul.53
  62.8 0.1 broadcast_in_dim.32
  62.9 0.1 mul.49
  63.0 0.1 broadcast_in_dim.33
  63.0 0.1 reshape.294
  63.1 0.7 gather_fusion.1
  63.9 0.2 convert_reduce_fusion
  64.1 0.2 fusion.9
  64.3 28.6 %all-gather.5.cloned.1.call-done = bf16[256,3584]{1,0:T(8,128)(2,1)} async-done(((bf16[64,3584]{1,0:T(8,128)(2,1)}), bf16[256,3584]{1,0:T(8,128)(2,1)}) %all-gather.5.cloned.1.call-update) | async-done | bytes 1835024 | tf_op jit(solution)/shard_map/all_gather | solution.py:104
  92.9 1.9 fusion.1
  94.8 0.1 select_reduce_fusion.1
  94.9 0.1 select_reduce_fusion
  95.0 94.9 %all-gather.7.cloned.1.call-done = bf16[3584,2560]{1,0:T(8,128)(2,1)} async-done(((bf16[448,2560]{1,0:T(8,128)(2,1)}), bf16[3584,2560]{1,0:T(8,128)(2,1)}) %all-gather.7.cloned.1.call-update) | async-done | bytes 18350096 | tf_op jit(solution)/shard_map/all_gather | solution.py:62
  190.0 0.0 copy-done.2
  190.0 12.8 %convolution_convert_fusion.2 = bf16[256,2560]{1,0:T(8,128)(2,1)} fusion(bf16[3584,2560]{1,0:T(8,128)(2,1)} %all-gather.7.cloned.1.call-done, bf16[256,3584]{1,0:T(8,128)(2,1)} %all-gather.5.cloned.1.call-done, f32[3584]{0:T(1024)S(1)} %copy-done.2, f32[256]{0:T(256)S(1)} %select_reduce_fusion), kind=kOutput, calls=%fused_computation.7 | convolution fusion | flops 4701945856 | bytes 21511168 | tf_op jit(solution)/shard_map/dot_general | solution.py:60
  (13 shorter events, 0.1 us)
Async XLA Ops:
  13.0 8.2 %copy-start = (s32[1,4]{1,0:T(1,128)S(1)}, s32[1,4]{1,0:T(1,128)}, u32[]{:S(2)}) copy-start(s32[1,4]{1,0:T(1,128)} %param.7) | copy-start | bytes 52
  14.9 29.8 %all-to-all-start = ((bf16[4,2,57344]{2,1,0:T(2,128)(2,1)}), bf16[4,2,57344]{2,1,0:T(2,128)(2,1)S(1)}, u32[]{:S(2)}, u32[]{:S(2)}) async-start(bf16[4,2,57344]{2,1,0:T(2,128)(2,1)} %reshape.328), calls=%async_computation | async-start | bytes 1835008 | tf_op jit(solution)/shard_map/all_to_all | solution.py:97
  21.2 71.7 %all-gather.5.cloned.1.call-start = ((), (), s32[]{:S(2)}) async-start(), calls=%async_computation.1 | async-start | bytes 2293760 | tf_op jit(solution)/shard_map/all_gather | solution.py:104
  46.8 2.0 copy-start.1
  48.1 141.9 %all-gather.7.cloned.1.call-start = ((), (), s32[]{:S(2)}) async-start(), calls=%async_computation.2 | async-start | bytes 20643840 | tf_op jit(solution)/shard_map/all_gather | solution.py:62
  48.8 141.2 %copy-start.2 = (f32[3584]{0:T(1024)S(1)}, f32[3584]{0:T(1024)}, u32[]{:S(2)}) copy-start(f32[3584]{0:T(1024)} %param.8) | copy-start | bytes 43012
Sparse Core Ops, SparseCore 0:
  48.2 44.6 all-gather.4
  94.8 95.1 all-gather.6
where the time goes:
time: 210 us
  waiting for transfers between devices  124 us (59%)
  blocking collectives  34.1 us (16%)
  matrix products  15.4 us (7%)
  between operations  13.5 us (6%)
  local copies, waits for them, and re-layouts  9.32 us (4%)
  other arithmetic  6.66 us (3%)
  starting transfers between devices  6.39 us (3%)
    all_gather x1, waiting for transfers between devices, fold_rows(): lax.all_gather(weight, 'dp', axis=0, tiled=True)  94.9 us
    all_gather x1, waiting for transfers between devices, per_device(): raw_all = lax.all_gather(owned_rows, 'grp', axis=0, tiled=True)  28.6 us
    all_gather x1, blocking collectives, per_device(): lax.all_gather(dest, 'grp', axis=0, tiled=True)  20.8 us
    all_gather x1, blocking collectives, per_device(): lax.all_gather(lengths, 'grp', axis=0, tiled=True)  13.2 us
    dot_general x1, matrix products, fold_rows(): jnp.dot(rows_all, lax.all_gather(weight, 'dp', axis=0, tiled=True), prefe...  12.8 us
    all_to_all x1, starting transfers between devices, per_device(): lax.all_to_all(parcel, 'grp', split_axis=0, concat_axis=0, tiled=True)  6.35 us
  transfers between devices with their start and end apart: 3, of which 2 were waited for; matrix products, arithmetic and copies ran while one was open for 3% of the time, Pallas kernels for 0%

commit v1 on v0

--- a/solution.py
+++ b/solution.py
@@ -6,6 +6,28 @@
 BLK = 32
 OWN_BLK = 2
 EPS = 1e-06
+
+
+def in_order(blocks, dim):
+    lengths = list(blocks.shape[1:])
+    lengths[dim] *= blocks.shape[0]
+    return jnp.moveaxis(blocks, 0, dim).reshape(lengths)
+
+
+def collect(x, axis, dim):
+    size = lax.axis_size(axis)
+    pairs = [(i, (i + 1) % size) for i in range(size)]
+    back = [(b, a) for a, b in pairs]
+    lower, upper = ([], [])
+    for lap in range(size - 1):
+        if lap % 2 == 0:
+            lower.append(lax.ppermute(lower[-1] if lower else x, axis, pairs))
+        else:
+            upper.append(lax.ppermute(upper[-1] if upper else x, axis, back))
+    parts = jnp.stack([*lower[::-1], x, *upper])
+    shift = lax.axis_index(axis) - len(lower)
+    parts = parts[(jnp.arange(size) - shift) % size]
+    return in_order(parts, dim)
 
 
 def group_layout(dest_all, own_blocks):
@@ -57,11 +79,9 @@
 
 
 def fold_rows(rows_all, weight):
-    return jnp.dot(
-        rows_all,
-        lax.all_gather(weight, "dp", axis=0, tiled=True),
-        preferred_element_type=jnp.float32,
-    ).astype(jnp.bfloat16)
+    return jnp.dot(rows_all, collect(weight, "dp", 0), preferred_element_type=jnp.float32).astype(
+        jnp.bfloat16
+    )
 
 
 def per_device(tokens, lengths, dest, gain, weight):

time: 210 us -> 238 us (1.13)
  the two profiles are of different devices: /device:TPU:0 before, /device:TPU:1 now
where the time goes in v1:
time: 238 us
  waiting for transfers between devices  107 us (45%)
  local copies, waits for them, and re-layouts  44.4 us (19%)
  blocking collectives  24.2 us (10%)
  starting transfers between devices  23.3 us (10%)
  other arithmetic  14.9 us (6%)
  between operations  13.6 us (6%)
  matrix products  10.1 us (4%)
    ppermute x4, waiting for transfers between devices, collect(): lower.append(lax.ppermute(lower[-1] if lower else x, axis, pairs))  91.3 us
    gather x3, local copies, waits for them, and re-layouts, collect(): parts = parts[(jnp.arange(size) - shift) % size]  24.3 us
    all_gather x1, blocking collectives, per_device(): lax.all_gather(dest, 'grp', axis=0, tiled=True)  17.6 us
    ppermute x3, waiting for transfers between devices, collect(): upper.append(lax.ppermute(upper[-1] if upper else x, axis, back))  14.8 us
    unnamed x19, local copies, waits for them, and re-layouts  13.4 us
    ppermute x4, starting transfers between devices, collect(): lower.append(lax.ppermute(lower[-1] if lower else x, axis, pairs))  9.92 us
    ppermute x3, starting transfers between devices, collect(): upper.append(lax.ppermute(upper[-1] if upper else x, axis, back))  8.77 us
    unnamed x1, other arithmetic  8.36 us
  transfers between devices with their start and end apart: 9, of which 7 were waited for; matrix products, arithmetic and copies ran while one was open for 13% of the time, Pallas kernels for 0%

profile of v1, /device:TPU:1, one launch (start us, length us, event | category | flops | bytes accessed | tf_op | source)
XLA Modules:
  0.0 237.6 jit_solution(7752534938134518612)
XLA Ops:
  6.5 2.6 %collective-permute-start = (bf16[448,2560]{1,0:T(8,128)(2,1)}, bf16[448,2560]{1,0:T(8,128)(2,1)}, u32[]{:S(2)}, u32[]{:S(2)}) collective-permute-start(bf16[448,2560]{1,0:T(8,128)(2,1)} %param.9), channel_id=1, source_target_pairs={{0,1},{1,2},{2,3},{3,4},{4,5},{5,6},{6,7},{7,0},{8,9},{9,10},{10,1... | collective-permute-start | bytes 6881288 | tf_op jit(solution)/shard_map/ppermute | solution.py:24
  9.1 25.4 %collective-permute-done = bf16[448,2560]{1,0:T(8,128)(2,1)} collective-permute-done((bf16[448,2560]{1,0:T(8,128)(2,1)}, bf16[448,2560]{1,0:T(8,128)(2,1)}, u32[]{:S(2)}, u32[]{:S(2)}) %collective-permute-start) | collective-permute-done | bytes 2293792 | tf_op jit(solution)/shard_map/ppermute | solution.py:24
  34.5 2.5 %collective-permute-start.1 = (bf16[448,2560]{1,0:T(8,128)(2,1)}, bf16[448,2560]{1,0:T(8,128)(2,1)}, u32[]{:S(2)}, u32[]{:S(2)}) collective-permute-start(bf16[448,2560]{1,0:T(8,128)(2,1)} %collective-permute-done), channel_id=1, source_target_pairs={{0,1},{1,2},{2,3},{3,4},{4,5},{5,6},{6,7},{7,0},{8,9},{9,10},{10,1... | collective-permute-start | bytes 6881288 | tf_op jit(solution)/shard_map/ppermute | solution.py:24
  37.0 0.0 collective-permute-start.4
  37.0 1.9 reshape.343
  38.9 0.9 convert_reduce_fusion.3
  39.8 1.3 fusion
  41.1 0.5 broadcast.438
  41.6 1.9 reduce.9
  43.5 1.9 reshape.397
  45.3 4.6 %all-to-all-start = ((bf16[4,2,57344]{2,1,0:T(2,128)(2,1)}), bf16[4,2,57344]{2,1,0:T(2,128)(2,1)S(1)}, u32[]{:S(2)}, u32[]{:S(2)}) async-start(bf16[4,2,57344]{2,1,0:T(2,128)(2,1)} %reshape.397), calls=%async_computation | async-start | bytes 1835008 | tf_op jit(solution)/shard_map/all_to_all | solution.py:117
  49.9 17.6 %all-gather = s32[4,1,4]{2,1,0:T(1,128)S(1)} all-gather(s32[1,1,4]{2,1,0:T(1,128)S(1)} %bitcast.41), channel_id=1, replica_groups=mesh['grp'=4,'dp'=8] {'grp'}, dimensions={0}, use_global_device_ids=true | all-gather | bytes 80 | tf_op jit(solution)/shard_map/all_gather | solution.py:94
  67.5 0.5 broadcast.436
  68.1 0.6 reduce.8
  68.6 0.1 eq.135
  68.7 0.2 convert_reduce_fusion.2
  68.9 16.2 %collective-permute-done.1 = bf16[448,2560]{1,0:T(8,128)(2,1)} collective-permute-done((bf16[448,2560]{1,0:T(8,128)(2,1)}, bf16[448,2560]{1,0:T(8,128)(2,1)}, u32[]{:S(2)}, u32[]{:S(2)}) %collective-permute-start.1) | collective-permute-done | bytes 2293792 | tf_op jit(solution)/shard_map/ppermute | solution.py:24
  85.1 2.5 %collective-permute-start.2 = (bf16[448,2560]{1,0:T(8,128)(2,1)}, bf16[448,2560]{1,0:T(8,128)(2,1)S(1)}, u32[]{:S(2)}, u32[]{:S(2)}) collective-permute-start(bf16[448,2560]{1,0:T(8,128)(2,1)} %collective-permute-done.1), channel_id=1, source_target_pairs={{0,1},{1,2},{2,3},{3,4},{4,5},{5,6},{6,7},{7,0},{8,9},{9,10},{10,1... | collective-permute-start | bytes 6881288 | tf_op jit(solution)/shard_map/ppermute | solution.py:24
  87.6 0.1 select_reduce_fusion.2
  87.7 0.2 dynamic-slice_reduce_fusion
  88.0 0.6 gather_fusion
  88.6 2.2 reshape.398
  90.9 2.8 %convolution_convert_fusion.1 = bf16[2,114688]{1,0:T(2,128)(2,1)S(1)} fusion(bf16[4,1,114688]{2,1,0:T(2,128)(2,1)} %reshape.398, s32[2]{0:T(128)S(1)} %fusion.24), kind=kOutput, calls=%fused_computation.6 | convolution fusion | flops 2064392 | bytes 1376264 | tf_op jit(solution)/shard_map/dot_general | solution.py:120
  93.7 1.2 reshape.344
  94.9 0.0 all-gather.4.cloned.1.call-update
  94.9 0.2 collective-permute-start.5
  95.1 32.2 %collective-permute-done.2 = bf16[448,2560]{1,0:T(8,128)(2,1)S(1)} collective-permute-done((bf16[448,2560]{1,0:T(8,128)(2,1)}, bf16[448,2560]{1,0:T(8,128)(2,1)S(1)}, u32[]{:S(2)}, u32[]{:S(2)}) %collective-permute-start.2) | collective-permute-done | bytes 2293792 | tf_op jit(solution)/shard_map/ppermute | solution.py:24
  127.3 2.4 collective-permute-start.3
  129.6 6.5 %all-gather.1 = s32[4,1,4]{2,1,0:T(1,128)S(1)} all-gather(s32[1,1,4]{2,1,0:T(1,128)S(1)} %bitcast.42), channel_id=1, replica_groups=mesh['grp'=4,'dp'=8] {'grp'}, dimensions={0}, use_global_device_ids=true | all-gather | bytes 80 | tf_op jit(solution)/shard_map/all_gather | solution.py:93
  136.2 0.1 copy.15
  136.3 0.1 reshape.345
  136.4 0.1 iota_add_fusion
  136.4 0.1 add.138
  136.5 0.1 add.145
  136.7 0.1 broadcast_in_dim.32
  136.7 0.1 mul.49
  136.8 0.2 reduce_window_sum.11
  137.0 0.1 broadcast_in_dim.33
  137.1 0.1 reshape.346
  137.2 0.1 mul.53
  137.3 0.7 gather_fusion.1
  138.0 0.2 convert_reduce_fusion
  138.2 0.2 fusion.9
  138.4 1.1 all-gather.4.cloned.1.call-done
  139.5 1.9 fusion.1
  141.4 0.1 select_reduce_fusion.1
  141.5 0.1 select_reduce_fusion
  141.6 2.3 collective-permute-done.5
  143.9 8.6 %collective-permute-start.6 = (bf16[448,2560]{1,0:T(8,128)(2,1)}, bf16[448,2560]{1,0:T(8,128)(2,1)S(1)}, u32[]{:S(2)}, u32[]{:S(2)}) collective-permute-start(bf16[448,2560]{1,0:T(8,128)(2,1)} %collective-permute-done.5), channel_id=1, source_target_pairs={{1,0},{2,1},{3,2},{4,3},{5,4},{6,5},{7,6},{0,7},{9,8},{10,9},{11,1... | collective-permute-start | bytes 6881288 | tf_op jit(solution)/shard_map/ppermute | solution.py:26
  152.5 17.5 %collective-permute-done.3 = bf16[448,2560]{1,0:T(8,128)(2,1)} collective-permute-done((bf16[448,2560]{1,0:T(8,128)(2,1)S(1)}, bf16[448,2560]{1,0:T(8,128)(2,1)}, u32[]{:S(2)}, u32[]{:S(2)}) %collective-permute-start.3) | collective-permute-done | bytes 2293792 | tf_op jit(solution)/shard_map/ppermute | solution.py:24
  170.0 1.8 bitcast_dynamic-update-slice_fusion.7
  171.8 0.1 bitcast_dynamic-update-slice_fusion.6
  172.0 1.8 bitcast_dynamic-update-slice_fusion.5
  173.8 1.8 bitcast_dynamic-update-slice_fusion.4
  175.6 0.1 bitcast_dynamic-update-slice_fusion.3
  175.8 1.8 bitcast_dynamic-update-slice_fusion.2
  177.6 1.8 bitcast_dynamic-update-slice_fusion.1
  179.4 12.5 %collective-permute-done.6 = bf16[448,2560]{1,0:T(8,128)(2,1)S(1)} collective-permute-done((bf16[448,2560]{1,0:T(8,128)(2,1)}, bf16[448,2560]{1,0:T(8,128)(2,1)S(1)}, u32[]{:S(2)}, u32[]{:S(2)}) %collective-permute-start.6) | collective-permute-done | bytes 2293792 | tf_op jit(solution)/shard_map/ppermute | solution.py:26
  191.9 0.1 bitcast_dynamic-update-slice_fusion
  192.0 6.9 %fusion.25 = (bf16[8,448,1280]{2,1,0:T(8,128)(2,1)}, bf16[8,448,1280]{2,1,0:T(8,128)(2,1)}) fusion(bf16[8,448,2560]{2,1,0:T(8,128)(2,1)S(1)} %bitcast_dynamic-update-slice_fusion), kind=kLoop, calls=%fused_computation.83 | loop fusion | bytes 36700160 | tf_op jit(solution)/shard_map/gather | solution.py:29
  199.0 8.7 %gather_fusion.3 = bf16[8,448,1280]{2,1,0:T(8,128)(2,1)} fusion(bf16[8,448,1280]{2,1,0:T(8,128)(2,1)} %get-tuple-element.10, s32[1024]{0:T(1024)S(1)} %get-tuple-element.12), kind=kCustom, calls=%fused_computation.3 | custom fusion | bytes 18350112 | tf_op jit(solution)/shard_map/gather | solution.py:29
  207.6 8.7 %gather_fusion.2 = bf16[8,448,1280]{2,1,0:T(8,128)(2,1)} fusion(bf16[8,448,1280]{2,1,0:T(8,128)(2,1)} %get-tuple-element.9, s32[1024]{0:T(1024)S(1)} %get-tuple-element.12), kind=kCustom, calls=%fused_computation.2 | custom fusion | bytes 18350112 | tf_op jit(solution)/shard_map/gather | solution.py:29
  216.4 8.4 %pad_maximum_fusion = bf16[8,448,2560]{2,1,0:T(8,128)(2,1)S(1)} fusion(bf16[8,448,1280]{2,1,0:T(8,128)(2,1)} %gather_fusion.3, bf16[8,448,1280]{2,1,0:T(8,128)(2,1)} %gather_fusion.2), kind=kLoop, calls=%fused_computation.7 | loop fusion | flops 36700160 | bytes 36700160
  224.8 6.0 %convolution_convert_fusion.2 = bf16[256,2560]{1,0:T(8,128)(2,1)} fusion(bf16[3584,2560]{1,0:T(8,128)(2,1)S(1)} %bitcast.35, bf16[256,3584]{1,0:T(8,128)(2,1)S(1)} %copy-done.1, f32[3584]{0:T(1024)S(1)} %copy-done.4, f32[256]{0:T(256)S(1)} %select_reduce_fusion), kind=kOutput, calls=%fused_computation.10 | convolution fusion | flops 4701945856 | bytes 21511168 | tf_op jit(solution)/shard_map/dot_general | solution.py:82
  (27 shorter events, 0.1 us)
Async XLA Ops:
  6.5 43.4 %copy-start.2 = (s32[1,4]{1,0:T(1,128)S(1)}, s32[1,4]{1,0:T(1,128)}, u32[]{:S(2)}) copy-start(s32[1,4]{1,0:T(1,128)} %param.7) | copy-start | bytes 52
  6.5 123.1 %copy-start.3 = (s32[1,4]{1,0:T(1,128)S(1)}, s32[1,4]{1,0:T(1,128)}, u32[]{:S(2)}) copy-start(s32[1,4]{1,0:T(1,128)} %param.6) | copy-start | bytes 52
  6.5 28.0 %collective-permute-start = (bf16[448,2560]{1,0:T(8,128)(2,1)}, bf16[448,2560]{1,0:T(8,128)(2,1)}, u32[]{:S(2)}, u32[]{:S(2)}) collective-permute-start(bf16[448,2560]{1,0:T(8,128)(2,1)} %param.9), channel_id=1, source_target_pairs={{0,1},{1,2},{2,3},{3,4},{4,5},{5,6},{6,7},{7,0},{8,9},{9,10},{10,1... | collective-permute-start | bytes 6881288 | tf_op jit(solution)/shard_map/ppermute | solution.py:24
  34.5 50.6 %collective-permute-start.1 = (bf16[448,2560]{1,0:T(8,128)(2,1)}, bf16[448,2560]{1,0:T(8,128)(2,1)}, u32[]{:S(2)}, u32[]{:S(2)}) collective-permute-start(bf16[448,2560]{1,0:T(8,128)(2,1)} %collective-permute-done), channel_id=1, source_target_pairs={{0,1},{1,2},{2,3},{3,4},{4,5},{5,6},{6,7},{7,0},{8,9},{9,10},{10,1... | collective-permute-start | bytes 6881288 | tf_op jit(solution)/shard_map/ppermute | solution.py:24
  37.0 57.9 %collective-permute-start.4 = (bf16[448,2560]{1,0:T(8,128)(2,1)}, bf16[448,2560]{1,0:T(8,128)(2,1)}, u32[]{:S(2)}, u32[]{:S(2)}) collective-permute-start(bf16[448,2560]{1,0:T(8,128)(2,1)} %param.9), channel_id=1, source_target_pairs={{1,0},{2,1},{3,2},{4,3},{5,4},{6,5},{7,6},{0,7},{9,8},{10,9},{11,1... | collective-permute-start | bytes 6881288 | tf_op jit(solution)/shard_map/ppermute | solution.py:26
  45.3 43.3 %all-to-all-start = ((bf16[4,2,57344]{2,1,0:T(2,128)(2,1)}), bf16[4,2,57344]{2,1,0:T(2,128)(2,1)S(1)}, u32[]{:S(2)}, u32[]{:S(2)}) async-start(bf16[4,2,57344]{2,1,0:T(2,128)(2,1)} %reshape.397), calls=%async_computation | async-start | bytes 1835008 | tf_op jit(solution)/shard_map/all_to_all | solution.py:117
  49.9 89.6 %all-gather.4.cloned.1.call-start = ((), (), s32[]{:S(2)}) async-start(), calls=%async_computation.1 | async-start | bytes 2293760 | tf_op jit(solution)/shard_map/all_gather | solution.py:124
  85.1 42.2 %collective-permute-start.2 = (bf16[448,2560]{1,0:T(8,128)(2,1)}, bf16[448,2560]{1,0:T(8,128)(2,1)S(1)}, u32[]{:S(2)}, u32[]{:S(2)}) collective-permute-start(bf16[448,2560]{1,0:T(8,128)(2,1)} %collective-permute-done.1), channel_id=1, source_target_pairs={{0,1},{1,2},{2,3},{3,4},{4,5},{5,6},{6,7},{7,0},{8,9},{9,10},{10,1... | collective-permute-start | bytes 6881288 | tf_op jit(solution)/shard_map/ppermute | solution.py:24
  94.9 49.0 %collective-permute-start.5 = (bf16[448,2560]{1,0:T(8,128)(2,1)}, bf16[448,2560]{1,0:T(8,128)(2,1)}, u32[]{:S(2)}, u32[]{:S(2)}) collective-permute-start(bf16[448,2560]{1,0:T(8,128)(2,1)} %collective-permute-done.4), channel_id=1, source_target_pairs={{1,0},{2,1},{3,2},{4,3},{5,4},{6,5},{7,6},{0,7},{9,8},{10,9},{11,1... | collective-permute-start | bytes 6881288 | tf_op jit(solution)/shard_map/ppermute | solution.py:26
  127.3 42.8 %collective-permute-start.3 = (bf16[448,2560]{1,0:T(8,128)(2,1)S(1)}, bf16[448,2560]{1,0:T(8,128)(2,1)}, u32[]{:S(2)}, u32[]{:S(2)}) collective-permute-start(bf16[448,2560]{1,0:T(8,128)(2,1)S(1)} %collective-permute-done.2), channel_id=1, source_target_pairs={{0,1},{1,2},{2,3},{3,4},{4,5},{5,6},{6,7},{7,0},{8,9},{9,10},{10,1... | collective-permute-start | bytes 6881288 | tf_op jit(solution)/shard_map/ppermute | solution.py:24
  141.6 34.0 %copy-start = (bf16[448,2560]{1,0:T(8,128)(2,1)S(1)}, bf16[448,2560]{1,0:T(8,128)(2,1)}, u32[]{:S(2)}) copy-start(bf16[448,2560]{1,0:T(8,128)(2,1)} %param.9) | copy-start | bytes 6881284
  143.9 47.9 %collective-permute-start.6 = (bf16[448,2560]{1,0:T(8,128)(2,1)}, bf16[448,2560]{1,0:T(8,128)(2,1)S(1)}, u32[]{:S(2)}, u32[]{:S(2)}) collective-permute-start(bf16[448,2560]{1,0:T(8,128)(2,1)} %collective-permute-done.5), channel_id=1, source_target_pairs={{1,0},{2,1},{3,2},{4,3},{5,4},{6,5},{7,6},{0,7},{9,8},{10,9},{11,1... | collective-permute-start | bytes 6881288 | tf_op jit(solution)/shard_map/ppermute | solution.py:26
  216.4 8.4 %copy-start.1 = (bf16[256,3584]{1,0:T(8,128)(2,1)S(1)}, bf16[256,3584]{1,0:T(8,128)(2,1)}, u32[]{:S(2)}) copy-start(bf16[256,3584]{1,0:T(8,128)(2,1)} %all-gather.4.cloned.1.call-done) | copy-start | bytes 5505028
  216.4 8.4 %copy-start.4 = (f32[3584]{0:T(1024)S(1)}, f32[3584]{0:T(1024)}, u32[]{:S(2)}) copy-start(f32[3584]{0:T(1024)} %param.8) | copy-start | bytes 43012
Sparse Core Ops, SparseCore 0:
  95.0 44.4 all-gather.3
